TPU v7x, 32 devices: a whole 2x2x4 slice. The times are simulated.
32 devices in a mesh: dp: 8 (over y, x, core), seq: 4 (over z).
Axes of the slice: x: 2, y: 2, z: 4, core: 2. Of those that a mesh axis runs over, the one named last changes fastest.
Arguments:
- grad_rows: bfloat16 [8, 320, 4, 1280], P('dp', 'seq'), may hold values from -6 to 6
- row_owner: int32 [8, 320, 1], P('dp', 'seq'), may hold values from 0 to 3; in each aligned block of 80 rows (0 to 79, 80 to 159, ..., all dimensions but the last counted through in order) at most 25 rows name the same one
- acts: bfloat16 [8, 4, 100, 4, 1280], P('dp', 'seq'), may hold values from -6 to 6
- xact: bfloat16 [8, 4, 100, 4, 1280], P('dp', 'seq'), may hold values from -72 to 72
- gamma: float32 [1280], replicated, may hold values from 0.25 to 1.75
- w_out: bfloat16 [1280, 1280], replicated, may hold values from -0.15625 to 0.15625
Outputs:
- attn_grad: bfloat16 [8, 4, 100, 4, 1280], P('dp', 'seq')
- weight_grad: float32 [1280, 1280], P('dp')
- gain_grad: float32 [1280], replicated
Inputs may be any that keep to these rules, and one draw needn't show every extreme that they name: `row_owner`: within the rows of one device (each aligned block of 80 rows) no owner is named more than 25 times, a bound that some block reaches.
All inputs are finite; a program needn't handle non-finite values.
Results may differ from a plain program's by a relative error of at most 0.0049.
Values may be sent and summed in bfloat16 or wider, within the bound.
A program may use at most 64 MiB of HBM per device.

v0:
```python
import jax
import jax.numpy as jnp
from jax import lax
from jax.sharding import PartitionSpec as P

epsilon = 1e-06


def slot_table(owners, buckets, capacity):
    picked = (owners[:, None] == jnp.arange(buckets, dtype=jnp.int32)[None, :]).astype(jnp.int32)
    before = jnp.cumsum(picked, axis=0) - picked
    ranking = jnp.sum(before * picked, axis=1)
    target = owners * capacity + ranking
    places = jnp.arange(buckets * capacity, dtype=jnp.int32)
    return (places[:, None] == target[None, :]).astype(jnp.bfloat16)


def norm_backward(upstream, inputs, gamma):
    values = inputs.astype(jnp.float32)
    inverse = lax.rsqrt(jnp.mean(values * values, axis=1, keepdims=True) + epsilon)
    normed = values * inverse
    gradient = upstream.astype(jnp.float32)
    gain_part = jnp.sum(gradient * normed, axis=0)
    scaled = gamma * gradient
    centre = jnp.mean(scaled * normed, axis=1, keepdims=True)
    patch_grad = (inverse * (scaled - normed * centre)).astype(jnp.bfloat16)
    return (patch_grad, gain_part)


def project_back(patch_grad, w_out):
    return lax.dot_general(
        patch_grad, w_out, (((1,), (1,)), ((), ())), preferred_element_type=jnp.float32
    ).astype(jnp.bfloat16)


def pick_rows(placing, stacked):
    return lax.dot_general(
        placing, stacked, (((0,), (0,)), ((), ())), preferred_element_type=jnp.float32
    ).astype(jnp.bfloat16)


def on_device(grad_rows, row_owner, acts, xact, gamma, w_out):
    seq_count = lax.axis_size("seq")
    slot_count = acts.shape[2]
    capacity = slot_count // seq_count
    patches = acts.shape[3]
    features = acts.shape[4]
    tok_rows = grad_rows.shape[1]
    placing = slot_table(row_owner[0, :, 0], seq_count, capacity)
    fetched = (
        lax.all_to_all(
            acts.reshape(seq_count, capacity, patches, features),
            "seq",
            split_axis=0,
            concat_axis=0,
            tiled=True,
        ),
        lax.all_to_all(
            xact.reshape(seq_count, capacity, patches, features),
            "seq",
            split_axis=0,
            concat_axis=0,
            tiled=True,
        ),
    )
    own_acts = pick_rows(placing, fetched[0].reshape(slot_count, patches * features))
    own_xact = pick_rows(placing, fetched[1].reshape(slot_count, patches * features))
    upstream = grad_rows.reshape(tok_rows * patches, features)
    act_rows = own_acts.reshape(tok_rows * patches, features)
    patch_grad, gain_part = norm_backward(
        upstream, own_xact.reshape(tok_rows * patches, features), gamma
    )
    attn_rows = project_back(patch_grad, w_out).reshape(tok_rows, patches * features)
    outgoing = jnp.dot(placing, attn_rows, preferred_element_type=jnp.float32).astype(jnp.bfloat16)
    returned = lax.all_to_all(
        outgoing.reshape(seq_count, capacity, patches, features),
        "seq",
        split_axis=0,
        concat_axis=0,
        tiled=True,
    )
    attn_grad = returned.reshape(acts.shape)
    weight_part = lax.psum_scatter(
        lax.dot_general(
            act_rows, patch_grad, (((0,), (0,)), ((), ())), preferred_element_type=jnp.float32
        ),
        "dp",
        scatter_dimension=0,
        tiled=True,
    )
    gain_sum = lax.psum(gain_part, ("dp", "seq"))
    weight_sum = lax.psum(weight_part, "seq")
    square_total = lax.psum(jnp.sum(weight_sum * weight_sum), "dp")
    norm_total = jnp.sqrt(square_total + jnp.sum(gain_sum * gain_sum) + epsilon)
    factor = jnp.float32(features) / norm_total
    return (attn_grad, weight_sum * factor, gain_sum * factor)


def solution(mesh):
    return jax.shard_map(
        on_device,
        mesh=mesh,
        in_specs=(
            P("dp", "seq", None, None),
            P("dp", "seq", None),
            P("dp", "seq", None, None, None),
            P("dp", "seq", None, None, None),
            P(),
            P(),
        ),
        out_specs=(P("dp", "seq", None, None, None), P("dp", None), P()),
        check_vma=False,
    )
```

profile of v0, /device:TPU:0, one launch (start us, length us, event | category | flops | bytes accessed | tf_op | source)
XLA Modules:
  0.0 224.4 jit_solution(17807708311614992503)
XLA Ops:
  7.2 0.0 copy-start
  7.2 0.0 copy-start.2
  7.2 6.6 %all-to-all-start = ((bf16[4,25,4,1280]{3,2,1,0:T(4,128)(2,1)}), bf16[4,25,4,1280]{3,2,1,0:T(4,128)(2,1)}, u32[]{:S(2)}, u32[]{:S(2)}) async-start(bf16[4,25,4,1280]{3,2,1,0:T(4,128)(2,1)} %bitcast.23), calls=%async_computation | async-start | bytes 2048000 | tf_op jit(solution)/shard_map/all_to_all | solution.py:58
  13.8 0.0 copy-done.2
  13.8 0.1 fusion.4
  13.9 0.1 reduce_window_sum.11
  14.0 25.1 %all-to-all-done = bf16[4,25,4,1280]{3,2,1,0:T(4,128)(2,1)} async-done(((bf16[4,25,4,1280]{3,2,1,0:T(4,128)(2,1)}), bf16[4,25,4,1280]{3,2,1,0:T(4,128)(2,1)}, u32[]{:S(2)}, u32[]{:S(2)}) %all-to-all-start) | async-done | bytes 1024032 | tf_op jit(solution)/shard_map/all_to_all | solution.py:58
  39.1 4.2 %all-to-all-start.2 = ((bf16[4,25,4,1280]{3,2,1,0:T(4,128)(2,1)}), bf16[4,25,4,1280]{3,2,1,0:T(4,128)(2,1)}, u32[]{:S(2)}, u32[]{:S(2)}) async-start(bf16[4,25,4,1280]{3,2,1,0:T(4,128)(2,1)} %bitcast.24), calls=%async_computation.2 | async-start | bytes 2048000 | tf_op jit(solution)/shard_map/all_to_all | solution.py:51
  43.4 0.0 reduce-scatter.2.cloned.1.call-start
  43.4 0.2 select_reduce_fusion
  43.6 1.6 pad
  45.2 0.1 copy.9
  45.4 1.6 fusion
  47.0 2.8 %reshape.145 = f32[320,1280]{1,0:T(8,128)} reshape(f32[80,5120]{1,0:T(8,128)} %fusion) | data formatting | bytes 3276800 | tf_op jit(solution)/shard_map/convert_element_type | solution.py:19
  49.8 3.0 %reshape.147 = f32[1,80,4,1280]{3,2,1,0:T(4,128)} reshape(f32[80,5120]{1,0:T(8,128)} %fusion) | data formatting | bytes 3276800 | tf_op jit(solution)/shard_map/convert_element_type | solution.py:19
  52.8 1.6 multiply_reduce_fusion.2
  54.5 0.1 rsqrt.14
  54.6 0.0 copy-done.1
  54.6 2.7 %multiply_reduce_fusion = (f32[1280]{0:T(1024)S(1)}, f32[80,4]{1,0:T(8,128)S(1)}) fusion(f32[1,80,4,1280]{3,2,1,0:T(4,128)} %reshape.147, bf16[1,80,4,1280]{3,2,1,0:T(4,128)(2,1)} %param.6, f32[80,4]{1,0:T(8,128)S(1)} %rsqrt.14, f32[1280]{0:T(1024)S(1)} %copy-done.1), kind=kLoop, calls=%fused_computation.5 | loop fusion | flops 2865600 | bytes 2470400 | tf_op jit(solution)/shard_map/reduce_sum | solution.py:23
  57.3 10.9 %all-to-all-done.2 = bf16[4,25,4,1280]{3,2,1,0:T(4,128)(2,1)} async-done(((bf16[4,25,4,1280]{3,2,1,0:T(4,128)(2,1)}), bf16[4,25,4,1280]{3,2,1,0:T(4,128)(2,1)}, u32[]{:S(2)}, u32[]{:S(2)}) %all-to-all-start.2) | async-done | bytes 1024032 | tf_op jit(solution)/shard_map/all_to_all | solution.py:51
  68.2 1.6 pad.1
  69.8 0.1 copy.10
  69.9 1.3 convolution_convert_fusion.1
  71.3 2.3 %reshape.144 = bf16[320,1280]{1,0:T(8,128)(2,1)} reshape(bf16[80,5120]{1,0:T(8,128)(2,1)} %convolution_convert_fusion.1) | data formatting | bytes 1638400 | tf_op jit(solution)/shard_map/reshape | solution.py:69
  73.6 3.3 %multiply_convert_fusion = bf16[1,80,4,1280]{3,2,1,0:T(4,128)(2,1)} fusion(f32[1,80,4,1280]{3,2,1,0:T(4,128)} %reshape.147, bf16[1,80,4,1280]{3,2,1,0:T(4,128)(2,1)} %param.6, f32[80,4]{1,0:T(8,128)S(1)} %broadcast_multiply_fusion.1, f32[80,4]{1,0:T(8,128)S(1)} %rsqrt.14, f32[1280]{0:T(1024)S(1)} %copy-done.1), kind=kLoop, calls=%fused_computation.6 | loop fusion | flops 2867200 | bytes 3284480 | tf_op jit(solution)/shard_map/convert_element_type | solution.py:26
  76.9 2.3 %convert_element_type.72 = bf16[320,1280]{1,0:T(8,128)(2,1)} reshape(bf16[1,80,4,1280]{3,2,1,0:T(4,128)(2,1)} %multiply_convert_fusion) | data formatting | bytes 1638400 | tf_op jit(solution)/shard_map/convert_element_type | solution.py:26
  79.2 6.0 %fusion.8 = f32[1280,1280]{1,0:T(8,128)} fusion(bf16[320,1280]{1,0:T(8,128)(2,1)} %reshape.144, bf16[320,1280]{1,0:T(8,128)(2,1)} %convert_element_type.72), kind=kOutput, calls=%fused_computation.27 | convolution fusion | flops 1048576000 | bytes 8192000 | tf_op jit(solution)/shard_map/dot_general | solution.py:84
  85.3 0.0 reduce-scatter.2.cloned.1.call-update
  85.3 2.6 %reshape.146 = f32[320,1280]{1,0:T(8,128)} reshape(bf16[1,80,4,1280]{3,2,1,0:T(4,128)(2,1)} %param.6) | data formatting | bytes 2457600 | tf_op jit(solution)/shard_map/convert_element_type | solution.py:22
  87.9 0.1 div.13
  88.0 0.0 copy-done
  88.0 4.2 %convolution_convert_fusion.3 = bf16[320,1280]{1,0:T(8,128)(2,1)} fusion(bf16[1280,1280]{1,0:T(8,128)(2,1)S(1)} %copy-done, f32[320,1280]{1,0:T(8,128)} %reshape.145, f32[320,1280]{1,0:T(8,128)} %reshape.146, f32[320]{0:T(512)S(1)} %div.13, f32[1280]{0:T(1024)S(1)} %copy-done.1, f32[320]{0:T(512)S(1)} %add_rsqrt_fusion), kind=kOutput, calls=%fused_computation.4 | convolution fusion | flops 1051443200 | bytes 7380480 | tf_op jit(solution)/shard_map/dot_general | solution.py:31
  92.2 2.4 %reshape.139 = bf16[80,5120]{1,0:T(8,128)(2,1)} reshape(bf16[320,1280]{1,0:T(8,128)(2,1)} %convolution_convert_fusion.3) | data formatting | bytes 1638400 | tf_op jit(solution)/shard_map/reshape | solution.py:73
  94.5 2.7 %convolution_convert_fusion = bf16[100,5120]{1,0:T(8,128)(2,1)} fusion(bf16[80,5120]{1,0:T(8,128)(2,1)} %reshape.139, s32[80]{0:T(128)S(1)} %multiply_add_fusion), kind=kOutput, calls=%fused_computation | convolution fusion | flops 82440000 | bytes 1843520 | tf_op jit(solution)/shard_map/dot_general | solution.py:74
  97.2 3.2 %reshape.140 = bf16[4,25,4,1280]{3,2,1,0:T(4,128)(2,1)} reshape(bf16[100,5120]{1,0:T(8,128)(2,1)} %convolution_convert_fusion) | data formatting | bytes 2048000 | tf_op jit(solution)/shard_map/reshape | solution.py:76
  100.4 4.2 %all-to-all-start.1 = ((bf16[4,25,4,1280]{3,2,1,0:T(4,128)(2,1)}), bf16[4,25,4,1280]{3,2,1,0:T(4,128)(2,1)}, u32[]{:S(2)}, u32[]{:S(2)}) async-start(bf16[4,25,4,1280]{3,2,1,0:T(4,128)(2,1)} %reshape.140), calls=%async_computation.1 | async-start | bytes 2048000 | tf_op jit(solution)/shard_map/all_to_all | solution.py:75
  104.7 0.0 all-reduce.2.cloned.1.call-start
  104.7 42.8 %reduce-scatter.2.cloned.1.call-done = f32[160,1280]{1,0:T(8,128)} async-done(((f32[1280,1280]{1,0:T(8,128)}), f32[160,1280]{1,0:T(8,128)}) %reduce-scatter.2.cloned.1.call-update) | async-done | bytes 819216 | tf_op jit(solution)/shard_map/reduce_scatter | solution.py:83
  147.5 0.0 all-reduce.2.cloned.1.call-update
  147.6 40.5 %psum.23 = f32[1280]{0:T(1024)S(1)} all-reduce(f32[1280]{0:T(1024)S(1)} %get-tuple-element.3), channel_id=1, replica_groups=mesh['dp'=8,'seq'=4] {'dp','seq'}, use_global_device_ids=true, to_apply=%region_9.10 | all-reduce | flops 1280 | bytes 10240 | tf_op jit(solution)/shard_map/psum | solution.py:91
  188.1 0.6 multiply_reduce_fusion.4
  188.7 6.7 %all-reduce.2.cloned.1.call-done = f32[160,1280]{1,0:T(8,128)} async-done(((f32[160,1280]{1,0:T(8,128)}), f32[160,1280]{1,0:T(8,128)}) %all-reduce.2.cloned.1.call-update) | async-done | bytes 819216 | tf_op jit(solution)/shard_map/psum | solution.py:92
  195.4 2.0 multiply_reduce_fusion.3
  197.3 0.0 all-to-all-done.1
  197.3 13.7 %psum.22 = f32[]{:T(128)} all-reduce(f32[]{:T(128)} %multiply_reduce_fusion.3), channel_id=1, replica_groups=mesh['dp'=8,'seq'=4] {'dp'}, use_global_device_ids=true, to_apply=%region_7.8 | all-reduce | flops 1 | bytes 8 | tf_op jit(solution)/shard_map/psum | solution.py:93
  212.4 0.6 broadcast_multiply_fusion.2
  213.0 2.1 broadcast_multiply_fusion
  215.1 2.5 %copy.13 = bf16[1,1,100,4,1280]{4,3,2,1,0:T(4,128)(2,1)} copy(bf16[1,1,100,4,1280]{4,3,2,1,0:T(4,128)(2,1)} %bitcast.2) | data formatting | bytes 2048000
  (4 shorter events, 0.0 us)
Async XLA Ops:
  7.2 80.8 %copy-start = (bf16[1280,1280]{1,0:T(8,128)(2,1)S(1)}, bf16[1280,1280]{1,0:T(8,128)(2,1)}, u32[]{:S(2)}) copy-start(bf16[1280,1280]{1,0:T(8,128)(2,1)} %param.11) | copy-start | bytes 9830404
  7.2 6.6 %copy-start.2 = (s32[1,80,1]{1,2,0:T(1,128)S(1)}, s32[1,80,1]{1,2,0:T(1,128)}, u32[]{:S(2)}) copy-start(s32[1,80,1]{1,2,0:T(1,128)} %param.7) | copy-start | bytes 964
  7.2 31.9 %all-to-all-start = ((bf16[4,25,4,1280]{3,2,1,0:T(4,128)(2,1)}), bf16[4,25,4,1280]{3,2,1,0:T(4,128)(2,1)}, u32[]{:S(2)}, u32[]{:S(2)}) async-start(bf16[4,25,4,1280]{3,2,1,0:T(4,128)(2,1)} %bitcast.23), calls=%async_computation | async-start | bytes 2048000 | tf_op jit(solution)/shard_map/all_to_all | solution.py:58
  39.1 29.1 %all-to-all-start.2 = ((bf16[4,25,4,1280]{3,2,1,0:T(4,128)(2,1)}), bf16[4,25,4,1280]{3,2,1,0:T(4,128)(2,1)}, u32[]{:S(2)}, u32[]{:S(2)}) async-start(bf16[4,25,4,1280]{3,2,1,0:T(4,128)(2,1)} %bitcast.24), calls=%async_computation.2 | async-start | bytes 2048000 | tf_op jit(solution)/shard_map/all_to_all | solution.py:51
  43.4 104.2 %reduce-scatter.2.cloned.1.call-start = ((), (), s32[]{:S(2)}) async-start(), calls=%async_computation.4 | async-start | bytes 7372800 | tf_op jit(solution)/shard_map/reduce_scatter | solution.py:83
  52.8 1.8 copy-start.1
  100.4 96.9 %all-to-all-start.1 = ((bf16[4,25,4,1280]{3,2,1,0:T(4,128)(2,1)}), bf16[4,25,4,1280]{3,2,1,0:T(4,128)(2,1)}, u32[]{:S(2)}, u32[]{:S(2)}) async-start(bf16[4,25,4,1280]{3,2,1,0:T(4,128)(2,1)} %reshape.140), calls=%async_computation.1 | async-start | bytes 2048000 | tf_op jit(solution)/shard_map/all_to_all | solution.py:75
  104.7 90.7 %all-reduce.2.cloned.1.call-start = ((), (), s32[]{:S(2)}) async-start(), calls=%async_computation.5 | async-start | bytes 1638400 | tf_op jit(solution)/shard_map/psum | solution.py:92
Sparse Core Ops, SparseCore 0:
  85.4 62.0 reduce-scatter.1
  149.9 45.4 all-reduce.1
where the time goes:
time: 225 us; the launch traced here: 224 us
  waiting for transfers between devices  85.5 us (38%)
  blocking collectives  54.2 us (24%)
  local copies, waits for them, and re-layouts  24.8 us (11%)
  matrix products  15.9 us (7%)
  between operations  15.5 us (7%)
  starting transfers between devices  15.2 us (7%)
  other arithmetic  13.3 us (6%)
    reduce_scatter x1, waiting for transfers between devices, on_device(): lax.psum_scatter(lax.dot_general(act_rows, patch_grad, (((0,), (0,)), (()...  42.8 us
    psum x1, blocking collectives, on_device(): gain_sum = lax.psum(gain_part, ('dp', 'seq'))  40.5 us
    all_to_all x1, waiting for transfers between devices, on_device(): lax.all_to_all(xact.reshape(seq_count, capacity, patches, features), 'seq...  25.1 us
    psum x1, blocking collectives, on_device(): square_total = lax.psum(jnp.sum(weight_sum * weight_sum), 'dp')  13.7 us
    all_to_all x1, waiting for transfers between devices, on_device(): lax.all_to_all(acts.reshape(seq_count, capacity, patches, features), 'seq...  10.9 us
    psum x1, waiting for transfers between devices, on_device(): weight_sum = lax.psum(weight_part, 'seq')  6.7 us
    all_to_all x1, starting transfers between devices, on_device(): lax.all_to_all(xact.reshape(seq_count, capacity, patches, features), 'seq...  6.62 us
    unnamed x11, local copies, waits for them, and re-layouts  6.05 us
  transfers between devices with their start and end apart: 5, of which 4 were waited for; matrix products, arithmetic and copies ran while one was open for 14% of the time, Pallas kernels for 0%

commit v1 on v0

--- a/solution.py
+++ b/solution.py
@@ -88,7 +88,8 @@
         scatter_dimension=0,
         tiled=True,
     )
-    gain_sum = lax.psum(gain_part, ("dp", "seq"))
+    parts = lax.all_gather(gain_part, ("dp", "seq"))
+    gain_sum = jnp.sum(parts, axis=0)
     weight_sum = lax.psum(weight_part, "seq")
     square_total = lax.psum(jnp.sum(weight_sum * weight_sum), "dp")
     norm_total = jnp.sqrt(square_total + jnp.sum(gain_sum * gain_sum) + epsilon)

time: 225 us -> 246 us (1.093)
  blocking collectives: 54.2 us -> 81.5 us
  waiting for transfers between devices: 85.5 us -> 78.8 us
    all_gather x0 -> x1, blocking collectives: none -> 69.1 us  [on_device(): parts = lax.all_gather(gain_part, ('dp', 'seq'))]
    psum x1 -> x0, blocking collectives: 40.5 us -> none  [on_device(): gain_sum = lax.psum(gain_part, ('dp', 'seq'))]
    psum x1, waiting for transfers between devices: 6.7 us -> 0.01 us  [on_device(): weight_sum = lax.psum(weight_part, 'seq')]
    unnamed x11 -> x12, local copies, waits for them, and re-layouts: 6.05 us -> 6.05 us
  transfers between devices with their start and end apart: 5 -> 5, of which waited for: 4 -> 3; matrix products, arithmetic and copies ran while one was open for 14% -> 13% of each run, Pallas kernels for 0% -> 0%
where the time goes in v1:
time: 246 us; the launch traced here: 245 us
  blocking collectives  81.5 us (33%)
  waiting for transfers between devices  78.8 us (32%)
  local copies, waits for them, and re-layouts  24.8 us (10%)
  matrix products  15.9 us (6%)
  between operations  15.5 us (6%)
  starting transfers between devices  15.2 us (6%)
  other arithmetic  13.5 us (5%)
    all_gather x1, blocking collectives, on_device(): parts = lax.all_gather(gain_part, ('dp', 'seq'))  69.1 us
    reduce_scatter x1, waiting for transfers between devices, on_device(): lax.psum_scatter(lax.dot_general(act_rows, patch_grad, (((0,), (0,)), (()...  42.8 us
    all_to_all x1, waiting for transfers between devices, on_device(): lax.all_to_all(xact.reshape(seq_count, capacity, patches, features), 'seq...  25.1 us
    psum x1, blocking collectives, on_device(): square_total = lax.psum(jnp.sum(weight_sum * weight_sum), 'dp')  12.4 us
    all_to_all x1, waiting for transfers between devices, on_device(): lax.all_to_all(acts.reshape(seq_count, capacity, patches, features), 'seq...  10.9 us
    all_to_all x1, starting transfers between devices, on_device(): lax.all_to_all(xact.reshape(seq_count, capacity, patches, features), 'seq...  6.62 us
    unnamed x12, local copies, waits for them, and re-layouts  6.05 us
    dot_general x1, matrix products, on_device(): lax.dot_general(act_rows, patch_grad, (((0,), (0,)), ((), ())), preferred...  6.03 us
  transfers between devices with their start and end apart: 5, of which 3 were waited for; matrix products, arithmetic and copies ran while one was open for 13% of the time, Pallas kernels for 0%

profile of v1, /device:TPU:0, one launch (start us, length us, event | category | flops | bytes accessed | tf_op | source)
XLA Modules:
  0.0 245.1 jit_solution(11323477373315361755)
XLA Ops:
  7.2 0.0 copy-start
  7.2 0.0 copy-start.2
  7.2 6.6 %all-to-all-start = ((bf16[4,25,4,1280]{3,2,1,0:T(4,128)(2,1)}), bf16[4,25,4,1280]{3,2,1,0:T(4,128)(2,1)}, u32[]{:S(2)}, u32[]{:S(2)}) async-start(bf16[4,25,4,1280]{3,2,1,0:T(4,128)(2,1)} %bitcast.23), calls=%async_computation | async-start | bytes 2048000 | tf_op jit(solution)/shard_map/all_to_all | solution.py:58
  13.8 0.0 copy-done.2
  13.8 0.1 fusion.4
  13.9 0.1 reduce_window_sum.11
  14.0 25.1 %all-to-all-done = bf16[4,25,4,1280]{3,2,1,0:T(4,128)(2,1)} async-done(((bf16[4,25,4,1280]{3,2,1,0:T(4,128)(2,1)}), bf16[4,25,4,1280]{3,2,1,0:T(4,128)(2,1)}, u32[]{:S(2)}, u32[]{:S(2)}) %all-to-all-start) | async-done | bytes 1024032 | tf_op jit(solution)/shard_map/all_to_all | solution.py:58
  39.1 4.2 %all-to-all-start.2 = ((bf16[4,25,4,1280]{3,2,1,0:T(4,128)(2,1)}), bf16[4,25,4,1280]{3,2,1,0:T(4,128)(2,1)}, u32[]{:S(2)}, u32[]{:S(2)}) async-start(bf16[4,25,4,1280]{3,2,1,0:T(4,128)(2,1)} %bitcast.24), calls=%async_computation.2 | async-start | bytes 2048000 | tf_op jit(solution)/shard_map/all_to_all | solution.py:51
  43.4 0.0 reduce-scatter.2.cloned.1.call-start
  43.4 0.2 select_reduce_fusion
  43.6 1.6 pad
  45.2 0.1 copy.9
  45.4 1.6 fusion
  47.0 2.8 %reshape.145 = f32[320,1280]{1,0:T(8,128)} reshape(f32[80,5120]{1,0:T(8,128)} %fusion) | data formatting | bytes 3276800 | tf_op jit(solution)/shard_map/convert_element_type | solution.py:19
  49.8 3.0 %reshape.147 = f32[1,80,4,1280]{3,2,1,0:T(4,128)} reshape(f32[80,5120]{1,0:T(8,128)} %fusion) | data formatting | bytes 3276800 | tf_op jit(solution)/shard_map/convert_element_type | solution.py:19
  52.8 1.6 multiply_reduce_fusion.2
  54.5 0.1 rsqrt.14
  54.6 0.0 copy-done.1
  54.6 2.7 %multiply_reduce_fusion = (f32[1280]{0:T(1024)S(1)}, f32[80,4]{1,0:T(8,128)S(1)}) fusion(f32[1,80,4,1280]{3,2,1,0:T(4,128)} %reshape.147, bf16[1,80,4,1280]{3,2,1,0:T(4,128)(2,1)} %param.6, f32[80,4]{1,0:T(8,128)S(1)} %rsqrt.14, f32[1280]{0:T(1024)S(1)} %copy-done.1), kind=kLoop, calls=%fused_computation.5 | loop fusion | flops 2865600 | bytes 2470400 | tf_op jit(solution)/shard_map/reduce_sum | solution.py:23
  57.3 10.9 %all-to-all-done.2 = bf16[4,25,4,1280]{3,2,1,0:T(4,128)(2,1)} async-done(((bf16[4,25,4,1280]{3,2,1,0:T(4,128)(2,1)}), bf16[4,25,4,1280]{3,2,1,0:T(4,128)(2,1)}, u32[]{:S(2)}, u32[]{:S(2)}) %all-to-all-start.2) | async-done | bytes 1024032 | tf_op jit(solution)/shard_map/all_to_all | solution.py:51
  68.2 1.6 pad.1
  69.8 0.1 copy.10
  69.9 1.3 convolution_convert_fusion.1
  71.3 2.3 reshape.144
  73.6 3.3 %multiply_convert_fusion = bf16[1,80,4,1280]{3,2,1,0:T(4,128)(2,1)} fusion(f32[1,80,4,1280]{3,2,1,0:T(4,128)} %reshape.147, bf16[1,80,4,1280]{3,2,1,0:T(4,128)(2,1)} %param.6, f32[80,4]{1,0:T(8,128)S(1)} %broadcast_multiply_fusion.1, f32[80,4]{1,0:T(8,128)S(1)} %rsqrt.14, f32[1280]{0:T(1024)S(1)} %copy-done.1), kind=kLoop, calls=%fused_computation.6 | loop fusion | flops 2867200 | bytes 3284480 | tf_op jit(solution)/shard_map/convert_element_type | solution.py:26
  76.9 2.3 convert_element_type.72
  79.2 6.0 %fusion.8 = f32[1280,1280]{1,0:T(8,128)} fusion(bf16[320,1280]{1,0:T(8,128)(2,1)} %reshape.144, bf16[320,1280]{1,0:T(8,128)(2,1)} %convert_element_type.72), kind=kOutput, calls=%fused_computation.27 | convolution fusion | flops 1048576000 | bytes 8192000 | tf_op jit(solution)/shard_map/dot_general | solution.py:84
  85.3 0.0 reduce-scatter.2.cloned.1.call-update
  85.3 2.6 %reshape.146 = f32[320,1280]{1,0:T(8,128)} reshape(bf16[1,80,4,1280]{3,2,1,0:T(4,128)(2,1)} %param.6) | data formatting | bytes 2457600 | tf_op jit(solution)/shard_map/convert_element_type | solution.py:22
  87.9 0.1 div.13
  88.0 0.0 copy-done
  88.0 4.2 %convolution_convert_fusion.3 = bf16[320,1280]{1,0:T(8,128)(2,1)} fusion(bf16[1280,1280]{1,0:T(8,128)(2,1)S(1)} %copy-done, f32[320,1280]{1,0:T(8,128)} %reshape.145, f32[320,1280]{1,0:T(8,128)} %reshape.146, f32[320]{0:T(512)S(1)} %div.13, f32[1280]{0:T(1024)S(1)} %copy-done.1, f32[320]{0:T(512)S(1)} %add_rsqrt_fusion), kind=kOutput, calls=%fused_computation.4 | convolution fusion | flops 1051443200 | bytes 7380480 | tf_op jit(solution)/shard_map/dot_general | solution.py:31
  92.2 2.4 reshape.139
  94.5 2.7 %convolution_convert_fusion = bf16[100,5120]{1,0:T(8,128)(2,1)} fusion(bf16[80,5120]{1,0:T(8,128)(2,1)} %reshape.139, s32[80]{0:T(128)S(1)} %multiply_add_fusion), kind=kOutput, calls=%fused_computation | convolution fusion | flops 82440000 | bytes 1843520 | tf_op jit(solution)/shard_map/dot_general | solution.py:74
  97.2 3.2 %reshape.140 = bf16[4,25,4,1280]{3,2,1,0:T(4,128)(2,1)} reshape(bf16[100,5120]{1,0:T(8,128)(2,1)} %convolution_convert_fusion) | data formatting | bytes 2048000 | tf_op jit(solution)/shard_map/reshape | solution.py:76
  100.4 4.2 %all-to-all-start.1 = ((bf16[4,25,4,1280]{3,2,1,0:T(4,128)(2,1)}), bf16[4,25,4,1280]{3,2,1,0:T(4,128)(2,1)}, u32[]{:S(2)}, u32[]{:S(2)}) async-start(bf16[4,25,4,1280]{3,2,1,0:T(4,128)(2,1)} %reshape.140), calls=%async_computation.1 | async-start | bytes 2048000 | tf_op jit(solution)/shard_map/all_to_all | solution.py:75
  104.7 0.0 all-reduce.2.cloned.1.call-start
  104.7 42.8 %reduce-scatter.2.cloned.1.call-done = f32[160,1280]{1,0:T(8,128)} async-done(((f32[1280,1280]{1,0:T(8,128)}), f32[160,1280]{1,0:T(8,128)}) %reduce-scatter.2.cloned.1.call-update) | async-done | bytes 819216 | tf_op jit(solution)/shard_map/reduce_scatter | solution.py:83
  147.5 0.0 all-reduce.2.cloned.1.call-update
  147.6 69.1 %all-gather.1 = f32[32,1,1280]{2,1,0:T(1,128)S(1)} all-gather(f32[1,1,1280]{2,1,0:T(1,128)S(1)} %reshape.149), channel_id=2, replica_groups=mesh['dp'=8,'seq'=4] {'dp','seq'}, dimensions={0}, use_global_device_ids=true | all-gather | bytes 168960 | tf_op jit(solution)/shard_map/all_gather | solution.py:91
  216.7 0.1 reduce_sum.68
  216.8 0.6 multiply_reduce_fusion.4
  217.4 2.0 multiply_reduce_fusion.3
  219.3 0.0 all-to-all-done.1
  219.3 12.4 %psum.15 = f32[]{:T(128)} all-reduce(f32[]{:T(128)} %multiply_reduce_fusion.3), channel_id=1, replica_groups=mesh['dp'=8,'seq'=4] {'dp'}, use_global_device_ids=true, to_apply=%region_7.8 | all-reduce | flops 1 | bytes 8 | tf_op jit(solution)/shard_map/psum | solution.py:94
  233.1 0.6 broadcast_multiply_fusion.2
  233.7 2.1 broadcast_multiply_fusion
  235.8 2.5 %copy.13 = bf16[1,1,100,4,1280]{4,3,2,1,0:T(4,128)(2,1)} copy(bf16[1,1,100,4,1280]{4,3,2,1,0:T(4,128)(2,1)} %bitcast.2) | data formatting | bytes 2048000
  (6 shorter events, 0.0 us)
Async XLA Ops:
  7.2 80.8 %copy-start = (bf16[1280,1280]{1,0:T(8,128)(2,1)S(1)}, bf16[1280,1280]{1,0:T(8,128)(2,1)}, u32[]{:S(2)}) copy-start(bf16[1280,1280]{1,0:T(8,128)(2,1)} %param.11) | copy-start | bytes 9830404
  7.2 6.6 %copy-start.2 = (s32[1,80,1]{1,2,0:T(1,128)S(1)}, s32[1,80,1]{1,2,0:T(1,128)}, u32[]{:S(2)}) copy-start(s32[1,80,1]{1,2,0:T(1,128)} %param.7) | copy-start | bytes 964
  7.2 31.9 %all-to-all-start = ((bf16[4,25,4,1280]{3,2,1,0:T(4,128)(2,1)}), bf16[4,25,4,1280]{3,2,1,0:T(4,128)(2,1)}, u32[]{:S(2)}, u32[]{:S(2)}) async-start(bf16[4,25,4,1280]{3,2,1,0:T(4,128)(2,1)} %bitcast.23), calls=%async_computation | async-start | bytes 2048000 | tf_op jit(solution)/shard_map/all_to_all | solution.py:58
  39.1 29.1 %all-to-all-start.2 = ((bf16[4,25,4,1280]{3,2,1,0:T(4,128)(2,1)}), bf16[4,25,4,1280]{3,2,1,0:T(4,128)(2,1)}, u32[]{:S(2)}, u32[]{:S(2)}) async-start(bf16[4,25,4,1280]{3,2,1,0:T(4,128)(2,1)} %bitcast.24), calls=%async_computation.2 | async-start | bytes 2048000 | tf_op jit(solution)/shard_map/all_to_all | solution.py:51
  43.4 104.2 %reduce-scatter.2.cloned.1.call-start = ((), (), s32[]{:S(2)}) async-start(), calls=%async_computation.4 | async-start | bytes 7372800 | tf_op jit(solution)/shard_map/reduce_scatter | solution.py:83
  52.8 1.8 copy-start.1
  100.4 118.9 %all-to-all-start.1 = ((bf16[4,25,4,1280]{3,2,1,0:T(4,128)(2,1)}), bf16[4,25,4,1280]{3,2,1,0:T(4,128)(2,1)}, u32[]{:S(2)}, u32[]{:S(2)}) async-start(bf16[4,25,4,1280]{3,2,1,0:T(4,128)(2,1)} %reshape.140), calls=%async_computation.1 | async-start | bytes 2048000 | tf_op jit(solution)/shard_map/all_to_all | solution.py:75
  104.7 112.7 %all-reduce.2.cloned.1.call-start = ((), (), s32[]{:S(2)}) async-start(), calls=%async_computation.5 | async-start | bytes 1638400 | tf_op jit(solution)/shard_map/psum | solution.py:93
Sparse Core Ops, SparseCore 0:
  85.4 62.0 reduce-scatter.1
  149.9 46.1 all-reduce.1
